TPU v7x, 32 devices: a whole 2x2x4 slice. The times are simulated.
32 devices in a mesh: unit: 4 (over y, core), zero: 4 (over z), cols: 2 (over x).
Axes of the slice: x: 2, y: 2, z: 4, core: 2. Of those that a mesh axis runs over, the one named last changes fastest.
Arguments:
- weight_gate: bfloat16 [20480, 13824], P(('unit', 'zero'), 'cols'), parts along dimension 0, may hold values from -0.125 to 0.125
- low_gate: bfloat16 [20480, 32], P(('unit', 'zero')), parts along dimension 0, may hold values from -0.078125 to 0.078125
- high_gate: bfloat16 [128, 13824], P('unit', 'cols'), parts along dimension 0, may hold values from -1 to 1
- weight_up: bfloat16 [20480, 13824], P(('unit', 'zero'), 'cols'), parts along dimension 0, may hold values from -0.125 to 0.125
- low_up: bfloat16 [20480, 32], P(('unit', 'zero')), parts along dimension 0, may hold values from -0.078125 to 0.078125
- high_up: bfloat16 [128, 13824], P('unit', 'cols'), parts along dimension 0, may hold values from -1 to 1
- norm_train: float32 [20480], P(('unit', 'zero', 'cols')), parts along dimension 0, may hold values from 0.25 to 1.75
- norm_step: float32 [20480], P(('unit', 'zero', 'cols')), parts along dimension 0, may hold values from -0.3 to 0.3
Outputs:
- final_gate: bfloat16 [20480, 13824], P('unit', ('cols', 'zero')), parts along dimension 0
- final_up: bfloat16 [20480, 13824], P('unit', ('cols', 'zero')), parts along dimension 0
- scale_gate: float32 [55296], P(('unit', 'cols', 'zero')), parts along dimension 0
- scale_up: float32 [55296], P(('unit', 'cols', 'zero')), parts along dimension 0
- serve_norm: bfloat16 [20480], P('unit'), parts along dimension 0
There are 4 independent parts, one for each index of `unit`. A program takes and returns all parts, laid end to end along the dimension named above; each array names one. Nothing has to cross between parts.
All inputs are finite; a program needn't handle non-finite values. Where the computation divides by a largest or mean magnitude, that divisor is 1e-20 or more.
Results may differ from a plain program's by a relative error of at most 0.001.
Values may be sent and summed in bfloat16 or wider, within the bound.
A program may use at most 192 MiB of HBM per device.

v0:
```python
import jax
import jax.numpy as jnp
from jax import lax
from jax.sharding import PartitionSpec as P

D_MODEL = 5120


mix_rate = 0.5


def local(weight_gate, low_gate, high_gate, weight_up, low_up, high_up, norm_train, norm_step):
    result_gate = weight_gate.astype(jnp.float32) + mix_rate * jnp.dot(
        low_gate, high_gate, preferred_element_type=jnp.float32
    )
    result_up = weight_up.astype(jnp.float32) + mix_rate * jnp.dot(
        low_up, high_up, preferred_element_type=jnp.float32
    )
    total_gate, total_up = lax.psum(
        (jnp.sum(jnp.abs(result_gate), axis=0), jnp.sum(jnp.abs(result_up), axis=0)), "zero"
    )
    scale_gate = total_gate / D_MODEL
    scale_up = total_up / D_MODEL
    narrow_gate, narrow_up = (
        (result_gate / scale_gate).astype(jnp.bfloat16),
        (result_up / scale_up).astype(jnp.bfloat16),
    )
    final_gate, final_up = (
        lax.all_to_all(narrow_gate, "zero", split_axis=1, concat_axis=0, tiled=True),
        lax.all_to_all(narrow_up, "zero", split_axis=1, concat_axis=0, tiled=True),
    )
    place = lax.axis_index("zero")
    scale_gate = lax.dynamic_slice_in_dim(
        scale_gate, place * final_gate.shape[1], final_gate.shape[1]
    )
    scale_up = lax.dynamic_slice_in_dim(scale_up, place * final_up.shape[1], final_up.shape[1])
    serve_norm = lax.all_gather(
        (norm_train + norm_step).astype(jnp.bfloat16), ("zero", "cols"), axis=0, tiled=True
    )
    return (final_gate, final_up, scale_gate, scale_up, serve_norm)


def solution(mesh):
    in_specs = (
        P(("unit", "zero"), "cols"),
        P(("unit", "zero"), None),
        P("unit", "cols"),
        P(("unit", "zero"), "cols"),
        P(("unit", "zero"), None),
        P("unit", "cols"),
        P(("unit", "zero", "cols")),
        P(("unit", "zero", "cols")),
    )
    out_specs = (
        P("unit", ("cols", "zero")),
        P("unit", ("cols", "zero")),
        P(("unit", "cols", "zero")),
        P(("unit", "cols", "zero")),
        P("unit"),
    )
    return jax.shard_map(local, mesh=mesh, in_specs=in_specs, out_specs=out_specs, check_vma=False)
```

profile of v0, /device:TPU:0, one launch (start us, length us, event | category | flops | bytes accessed | tf_op | source)
XLA Modules:
  0.0 996.0 jit_solution(447909113472326274)
XLA Ops:
  0.6 0.0 copy-start
  0.6 0.0 copy-start.3
  0.7 0.0 copy-start.2
  0.7 1.0 copy-done
  1.7 17.9 %abs_reduce_fusion.1 = (f32[6912]{0:T(1024)S(1)}, f32[1280,6912]{1,0:T(8,128)}) fusion(bf16[1280,32]{0,1:T(8,128)(2,1)} %param.9, bf16[32,6912]{1,0:T(8,128)(2,1)S(1)} %copy-done, bf16[1280,6912]{1,0:T(8,128)(2,1)} %param.8), kind=kOutput, calls=%fused_computation.4 | convolution fusion | flops 610460928 | bytes 53636096 | tf_op jit(solution)/shard_map/dot_general | solution.py:13
  19.6 0.0 copy-done.3
  19.6 0.0 copy-done.2
  19.6 18.0 %abs_reduce_fusion = (f32[6912]{0:T(1024)S(1)}, f32[1280,6912]{1,0:T(8,128)}) fusion(bf16[1280,32]{0,1:T(8,128)(2,1)S(1)} %copy-done.3, bf16[32,6912]{1,0:T(8,128)(2,1)S(1)} %copy-done.2, bf16[1280,6912]{1,0:T(8,128)(2,1)} %param.11), kind=kOutput, calls=%fused_computation.1 | convolution fusion | flops 610460928 | bytes 53636096 | tf_op jit(solution)/shard_map/dot_general | solution.py:16
  37.6 21.7 %all-reduce = (f32[6912]{0:T(1024)S(1)}, f32[6912]{0:T(1024)S(1)}) all-reduce(f32[6912]{0:T(1024)S(1)} %get-tuple-element.17, f32[6912]{0:T(1024)S(1)} %get-tuple-element.19), channel_id=1, replica_groups=mesh['unit'=4,'zero'=4,'cols'=2] {'zero'}, use_global_device_ids=true, to_apply=%region_1.0 | all-reduce | flops 13824 | bytes 110592 | tf_op jit(solution)/shard_map/psum | solution.py:19
  59.3 19.8 %divide_convert_fusion.1 = bf16[1280,6912]{1,0:T(8,128)(2,1)} fusion(f32[1280,6912]{1,0:T(8,128)} %get-tuple-element.18, f32[6912]{0:T(1024)S(1)} %get-tuple-element.22), kind=kLoop, calls=%fused_computation.3 | loop fusion | flops 17694720 | bytes 53111808 | tf_op jit(solution)/shard_map/convert_element_type | solution.py:25
  79.1 24.6 %copy.23 = bf16[1280,6912]{0,1:T(8,128)(2,1)} copy(bf16[1280,6912]{1,0:T(8,128)(2,1)} %divide_convert_fusion.1) | data formatting | bytes 35389440 | tf_op jit(solution)/shard_map/convert_element_type | solution.py:25
  103.7 7.2 all-to-all-start
  110.9 19.8 %divide_convert_fusion = bf16[1280,6912]{1,0:T(8,128)(2,1)} fusion(f32[1280,6912]{1,0:T(8,128)} %get-tuple-element.20, f32[6912]{0:T(1024)S(1)} %get-tuple-element.21), kind=kLoop, calls=%fused_computation | loop fusion | flops 17694720 | bytes 53111808 | tf_op jit(solution)/shard_map/convert_element_type | solution.py:26
  130.7 0.0 copy-start.4
  130.7 0.0 copy-start.5
  130.7 23.0 %copy.25 = bf16[1280,6912]{0,1:T(8,128)(2,1)} copy(bf16[1280,6912]{1,0:T(8,128)(2,1)} %divide_convert_fusion) | data formatting | bytes 35389440 | tf_op jit(solution)/shard_map/convert_element_type | solution.py:26
  153.7 335.9 %all-to-all-done = bf16[1280,4,1728]{0,2,1:T(8,128)(2,1)} async-done(((bf16[1280,4,1728]{0,2,1:T(8,128)(2,1)}), bf16[1280,4,1728]{0,2,1:T(8,128)(2,1)}, u32[]{:S(2)}, u32[]{:S(2)}) %all-to-all-start) | async-done | bytes 17694752 | tf_op jit(solution)/shard_map/all_to_all | solution.py:29
  489.6 7.2 all-to-all-start.1
  496.8 0.7 dynamic_slice.6
  497.5 0.7 dynamic_slice.7
  498.2 0.0 copy-done.4
  498.2 0.0 copy-done.5
  498.2 400.5 %all-gather = bf16[8,1,640]{2,1,0:T(2,128)(2,1)S(1)} all-gather(bf16[1,1,640]{2,1,0:T(2,128)(2,1)S(1)} %reshape.18), channel_id=1, replica_groups=mesh['unit'=4,'zero'=4,'cols'=2] {'zero','cols'}, dimensions={0}, use_global_device_ids=true | all-gather | bytes 11520 | tf_op jit(solution)/shard_map/all_gather | solution.py:37
  898.8 0.1 reduce
  898.8 0.6 reshape.19
  899.4 23.3 %copy.24 = bf16[4,1280,1728]{2,1,0:T(8,128)(2,1)} copy(bf16[4,1280,1728]{1,2,0:T(8,128)(2,1)} %bitcast.1) | data formatting | bytes 35389440 | tf_op jit(solution)/shard_map/all_to_all | solution.py:29
  922.8 24.9 %copy.27 = bf16[5120,1728]{0,1:T(8,128)(2,1)} copy(bf16[5120,1728]{1,0:T(8,128)(2,1)} %bitcast.10) | data formatting | bytes 35389440
  947.7 0.0 all-to-all-done.1
  947.7 0.0 copy-start.1
  947.7 23.4 %copy.26 = bf16[4,1280,1728]{2,1,0:T(8,128)(2,1)} copy(bf16[4,1280,1728]{1,2,0:T(8,128)(2,1)} %bitcast.4) | data formatting | bytes 35389440 | tf_op jit(solution)/shard_map/all_to_all | solution.py:30
  971.1 24.9 %copy.28 = bf16[5120,1728]{0,1:T(8,128)(2,1)} copy(bf16[5120,1728]{1,0:T(8,128)(2,1)} %bitcast.11) | data formatting | bytes 35389440
  996.0 0.0 copy-done.1
  (3 shorter events, 0.0 us)
Async XLA Ops:
  0.6 1.0 copy-start
  0.6 18.9 %copy-start.3 = (bf16[1280,32]{0,1:T(8,128)(2,1)S(1)}, bf16[1280,32]{0,1:T(8,128)(2,1)}, u32[]{:S(2)}) copy-start(bf16[1280,32]{0,1:T(8,128)(2,1)} %param.12) | copy-start | bytes 245764
  0.7 18.9 %copy-start.2 = (bf16[32,6912]{1,0:T(8,128)(2,1)S(1)}, bf16[32,6912]{1,0:T(8,128)(2,1)}, u32[]{:S(2)}) copy-start(bf16[32,6912]{1,0:T(8,128)(2,1)} %param.13) | copy-start | bytes 1327108
  103.7 385.9 %all-to-all-start = ((bf16[1280,4,1728]{0,2,1:T(8,128)(2,1)}), bf16[1280,4,1728]{0,2,1:T(8,128)(2,1)}, u32[]{:S(2)}, u32[]{:S(2)}) async-start(bf16[1280,4,1728]{0,2,1:T(8,128)(2,1)} %bitcast.13), calls=%async_computation | async-start | bytes 35389440 | tf_op jit(solution)/shard_map/all_to_all | solution.py:29
  130.7 367.5 %copy-start.4 = (f32[640]{0:T(1024)S(1)}, f32[640]{0:T(1024)}, u32[]{:S(2)}) copy-start(f32[640]{0:T(1024)} %param.14) | copy-start | bytes 7684
  130.7 367.5 %copy-start.5 = (f32[640]{0:T(1024)S(1)}, f32[640]{0:T(1024)}, u32[]{:S(2)}) copy-start(f32[640]{0:T(1024)} %param.15) | copy-start | bytes 7684
  489.6 458.1 %all-to-all-start.1 = ((bf16[1280,4,1728]{0,2,1:T(8,128)(2,1)}), bf16[1280,4,1728]{0,2,1:T(8,128)(2,1)}, u32[]{:S(2)}, u32[]{:S(2)}) async-start(bf16[1280,4,1728]{0,2,1:T(8,128)(2,1)} %bitcast.12), calls=%async_computation.1 | async-start | bytes 35389440 | tf_op jit(solution)/shard_map/all_to_all | solution.py:30
  947.7 48.3 %copy-start.1 = (bf16[32,6912]{1,0:T(8,128)(2,1)S(1)}, bf16[32,6912]{1,0:T(8,128)(2,1)}, u32[]{:S(2)}) copy-start(bf16[32,6912]{1,0:T(8,128)(2,1)} %param.10) | copy-start | bytes 1327108
where the time goes:
time: 1000 us; the launch traced here: 996 us
  blocking collectives  422 us (42%)
  waiting for transfers between devices  336 us (34%)
  local copies, waits for them, and re-layouts  147 us (15%)
  other arithmetic  39.7 us (4%)
  matrix products  35.9 us (4%)
  starting transfers between devices  14.4 us (1%)
    all_gather x1, blocking collectives, local(): lax.all_gather((norm_train + norm_step).astype(jnp.bfloat16), ('zero', 'c...  401 us
    all_to_all x1, waiting for transfers between devices, local(): lax.all_to_all(narrow_gate, 'zero', split_axis=1, concat_axis=0, tiled=True)  336 us
    unnamed x16, local copies, waits for them, and re-layouts  51.5 us
    convert_element_type x1, local copies, waits for them, and re-layouts, local(): (result_gate / scale_gate).astype(jnp.bfloat16)  24.6 us
    all_to_all x1, local copies, waits for them, and re-layouts, local(): lax.all_to_all(narrow_up, 'zero', split_axis=1, concat_axis=0, tiled=True)  23.4 us
    all_to_all x1, local copies, waits for them, and re-layouts, local(): lax.all_to_all(narrow_gate, 'zero', split_axis=1, concat_axis=0, tiled=True)  23.3 us
    convert_element_type x1, local copies, waits for them, and re-layouts, local(): (result_up / scale_up).astype(jnp.bfloat16)  23 us
    psum x1, blocking collectives, local(): lax.psum((jnp.sum(jnp.abs(result_gate), axis=0), jnp.sum(jnp.abs(result_u...  21.7 us
  transfers between devices with their start and end apart: 2, of which 1 were waited for; matrix products, arithmetic and copies ran while one was open for 9% of the time, Pallas kernels for 0%

commit v1 on v0

v1 whole, which is shorter than its diff:
```python
import jax
import jax.numpy as jnp
from jax import lax
from jax.experimental import pallas as pl
from jax.experimental.pallas import tpu as pltpu
from jax.sharding import PartitionSpec as P

mix_rate = 0.5


def cuts(units, shares):
    total, marks, seen = sum(shares), [0], 0
    for share in shares:
        seen += share
        marks.append(units * seen // total)
    return [(a, b) for a, b in zip(marks[:-1], marks[1:]) if b > a]


def merge_kernel(block_ref, low_ref, high_ref, *refs):
    final_ref, scale_ref, result_ref = refs[-3:]
    n, _, rows = block_ref.shape
    change = mix_rate * jnp.dot(high_ref[...], low_ref[...], preferred_element_type=jnp.float32)
    total = None
    for s in range(n):
        part = block_ref[s].astype(jnp.float32) + change[:, s * rows : (s + 1) * rows]
        result_ref[:, s * rows : (s + 1) * rows] = part
        size = jnp.sum(jnp.abs(part), axis=1, keepdims=True)
        total = size if total is None else total + size
    scale = total / (n * rows)
    scale_ref[...] = scale
    final_ref[...] = (result_ref[...] / scale).astype(final_ref.dtype)


def merge(block, low, high, final, first, step, width):
    n, part, rows = block.shape
    rank = low.shape[0]
    offset = first // step
    operands = [block, low, high]
    in_specs = [
        pl.BlockSpec((n, step, rows), lambda i: (0, i, 0)),
        pl.BlockSpec((rank, n * rows), lambda i: (0, 0)),
        pl.BlockSpec((step, rank), lambda i: (i + offset, 0)),
    ]
    aliases = {}
    if final is not None:
        operands.append(final)
        in_specs.append(pl.BlockSpec(memory_space=pl.ANY))
        aliases = {3: 0}
    return pl.pallas_call(
        merge_kernel,
        grid=(part // step,),
        in_specs=in_specs,
        out_specs=[
            pl.BlockSpec((step, n * rows), lambda i: (i + offset, 0)),
            pl.BlockSpec((step, 1), lambda i: (i, 0)),
        ],
        out_shape=[
            jax.ShapeDtypeStruct((width, n * rows), jnp.bfloat16),
            jax.ShapeDtypeStruct((part, 1), jnp.float32),
        ],
        scratch_shapes=[pltpu.VMEM((step, n * rows), jnp.float32)],
        input_output_aliases=aliases,
        cost_estimate=pl.CostEstimate(
            flops=2 * part * n * rows * rank,
            bytes_accessed=4 * part * n * rows,
            transcendentals=0,
        ),
        compiler_params=pltpu.CompilerParams(vmem_limit_bytes=24 << 20),
    )(*operands)


def local(weight_gate, low_gate, high_gate, weight_up, low_up, high_up, norm_train, norm_step):
    n = lax.axis_size("zero")
    rows, width = weight_gate.shape[0], weight_gate.shape[1] // n
    rank = low_gate.shape[1]
    place = lax.axis_index("zero")
    step = next(s for s in (48, 24, 16, 8, width) if width % s == 0)

    lows = lax.all_gather(
        jnp.concatenate([low_gate.T, low_up.T], axis=0), "zero", axis=1, tiled=True
    )
    serve_norm = lax.all_gather(
        (norm_train + norm_step).astype(jnp.bfloat16), ("zero", "cols"), axis=0, tiled=True
    )
    lows, serve_norm, weight_gate, weight_up = lax.optimization_barrier(
        (lows, serve_norm, weight_gate, weight_up)
    )
    low = {"gate": lows[:rank], "up": lows[rank:]}
    high = {
        "gate": lax.dynamic_slice_in_dim(high_gate, place * width, width, axis=1).T,
        "up": lax.dynamic_slice_in_dim(high_up, place * width, width, axis=1).T,
    }
    turned = {
        "gate": weight_gate.T.reshape(n, width, rows),
        "up": weight_up.T.reshape(n, width, rows),
    }

    shares = {"gate": (1, 3), "up": (7, 2)}
    jobs = [
        (name, a * step, b * step)
        for name in ("gate", "up")
        for a, b in cuts(width // step, shares[name])
    ]
    finals = {"gate": None, "up": None}
    scales = {"gate": [], "up": []}
    block = None
    arrived = []
    for name, a, b in jobs:
        sent = turned[name][:, a:b]
        if block is not None:
            sent, block = lax.optimization_barrier((sent, block))
            arrived.append(block)
        block = lax.all_to_all(sent, "zero", split_axis=0, concat_axis=0, tiled=True)
    arrived.append(block)
    for (name, a, b), block in zip(jobs, arrived):
        finals[name], scale = merge(block, low[name], high[name], finals[name], a, step, width)
        scales[name].append(scale[:, 0])
    return (
        finals["gate"].T,
        finals["up"].T,
        jnp.concatenate(scales["gate"]),
        jnp.concatenate(scales["up"]),
        serve_norm,
    )


def solution(mesh):
    in_specs = (
        P(("unit", "zero"), "cols"),
        P(("unit", "zero"), None),
        P("unit", "cols"),
        P(("unit", "zero"), "cols"),
        P(("unit", "zero"), None),
        P("unit", "cols"),
        P(("unit", "zero", "cols")),
        P(("unit", "zero", "cols")),
    )
    out_specs = (
        P("unit", ("cols", "zero")),
        P("unit", ("cols", "zero")),
        P(("unit", "cols", "zero")),
        P(("unit", "cols", "zero")),
        P("unit"),
    )
    return jax.shard_map(local, mesh=mesh, in_specs=in_specs, out_specs=out_specs, check_vma=False)
```

time: 1000 us -> 879 us (0.88)
  blocking collectives: 422 us -> 50.1 us
  waiting for transfers between devices: 336 us -> 647 us
  Pallas kernels: 0 us -> 66.6 us
  local copies, waits for them, and re-layouts: 147 us -> 83.8 us
  matrix products: 35.9 us -> 0 us
  other arithmetic: 39.7 us -> 3.89 us
    all_gather x1, blocking collectives: 401 us -> 30.4 us  [local(): lax.all_gather((norm_train + norm_step).astype(jnp.bfloat16), ('zero', 'c...]
    all_to_all x2 -> x4, waiting for transfers between devices: 336 us -> 647 us  [local(): lax.all_to_all(sent, 'zero', split_axis=0, concat_axis=0, tiled=True)]
    pallas_call x0 -> x4, Pallas kernels: none -> 66.6 us  [merge(): pl.pallas_call(merge_kernel, grid=(part // step,), in_specs=in_specs, out...]
    unnamed x16 -> x3, local copies, waits for them, and re-layouts: 51.5 us -> 0.55 us
    transpose x0 -> x2, local copies, waits for them, and re-layouts: none -> 49.2 us  [the longest x1 24.6 us: local(): weight_up.T.reshape(n, width, rows)]
    convert_element_type x2 -> x0, local copies, waits for them, and re-layouts: 47.6 us -> none  [the longest x1 24.6 us: local(): (result_gate / scale_gate).astype(jnp.bfloat16)]
    all_to_all x2 -> x0, local copies, waits for them, and re-layouts: 46.7 us -> none  [the longest x1 23.4 us: local(): lax.all_to_all(narrow_up, 'zero', split_axis=1, concat_axis=0, tiled=True)]
    convert_element_type x2 -> x0, other arithmetic: 39.6 us -> none  [the longest x1 19.8 us: local(): (result_up / scale_up).astype(jnp.bfloat16)]
  transfers between devices with their start and end apart: 2 -> 4, of which waited for: 1 -> 4; matrix products, arithmetic and copies ran while one was open for 9% -> 6% of each run, Pallas kernels for 0% -> 7%
where the time goes in v1:
time: 879 us; the launch traced here: 875 us
  waiting for transfers between devices  647 us (74%)
  local copies, waits for them, and re-layouts  83.8 us (10%)
  Pallas kernels  66.6 us (8%)
  blocking collectives  50.1 us (6%)
  starting transfers between devices  22.6 us (3%)
    all_to_all x4, waiting for transfers between devices, local(): lax.all_to_all(sent, 'zero', split_axis=0, concat_axis=0, tiled=True)  647 us
    pallas_call x4, Pallas kernels, merge(): pl.pallas_call(merge_kernel, grid=(part // step,), in_specs=in_specs, out...  66.6 us
    slice x4, local copies, waits for them, and re-layouts, local(): sent = turned[name][:, a:b]  32.3 us
    all_gather x1, blocking collectives, local(): lax.all_gather((norm_train + norm_step).astype(jnp.bfloat16), ('zero', 'c...  30.4 us
    transpose x1, local copies, waits for them, and re-layouts, local(): weight_up.T.reshape(n, width, rows)  24.6 us
    transpose x1, local copies, waits for them, and re-layouts, local(): weight_gate.T.reshape(n, width, rows)  24.6 us
    all_to_all x4, starting transfers between devices, local(): lax.all_to_all(sent, 'zero', split_axis=0, concat_axis=0, tiled=True)  22.6 us
    all_gather x1, blocking collectives, local(): lax.all_gather(jnp.concatenate([low_gate.T, low_up.T], axis=0), 'zero', a...  19.7 us
  transfers between devices with their start and end apart: 4, of which 4 were waited for; matrix products, arithmetic and copies ran while one was open for 6% of the time, Pallas kernels for 7%

profile of v1, /device:TPU:0, one launch (start us, length us, event | category | flops | bytes accessed | tf_op | source)
XLA Modules:
  0.0 875.1 jit_solution(18427595097443538595)
XLA Ops:
  0.6 0.9 pad_maximum_fusion
  1.6 19.7 %all_gather.6 = bf16[64,5120]{1,0:T(8,128)(2,1)S(1)} all-gather(bf16[64,1280]{1,0:T(8,128)(2,1)S(1)} %pad_maximum_fusion), channel_id=1, replica_groups=mesh['unit'=4,'zero'=4,'cols'=2] {'zero'}, dimensions={1}, use_global_device_ids=true | all-gather | bytes 819200 | tf_op jit(solution)/shard_map/all_gather | solution.py:79
  21.3 0.7 add_convert_fusion
  22.0 30.4 %all-gather = bf16[8,1,640]{2,1,0:T(2,128)(2,1)S(1)} all-gather(bf16[1,1,640]{2,1,0:T(2,128)(2,1)S(1)} %reshape.18), channel_id=1, replica_groups=mesh['unit'=4,'zero'=4,'cols'=2] {'zero','cols'}, dimensions={0}, use_global_device_ids=true | all-gather | bytes 11520 | tf_op jit(solution)/shard_map/all_gather | solution.py:82
  52.4 0.1 reduce
  52.5 0.6 reshape.19
  53.1 24.6 %copy.24 = bf16[6912,1280]{1,0:T(8,128)(2,1)} copy(bf16[6912,1280]{0,1:T(8,128)(2,1)} %bitcast.20) | data formatting | bytes 35389440 | tf_op jit(solution)/shard_map/transpose | solution.py:94
  77.7 4.6 slice.26
  82.4 4.9 all-to-all-start
  87.2 10.8 %slice.25 = bf16[4,1296,1280]{2,1,0:T(8,128)(2,1)} slice(bf16[4,1728,1280]{2,1,0:T(8,128)(2,1)} %bitcast.15), slice={[0:4], [432:1728], [0:1280]} | slice | bytes 26542080 | tf_op jit(solution)/shard_map/slice | solution.py:109
  98.1 78.3 %all-to-all-done.block_ref = bf16[4,432,1280]{2,1,0:T(8,128)(2,1)} async-done(((bf16[4,432,1280]{2,1,0:T(8,128)(2,1)}), bf16[4,432,1280]{2,1,0:T(8,128)(2,1)}, u32[]{:S(2)}, u32[]{:S(2)}) %all-to-all-start) | async-done | bytes 4423712 | tf_op jit(solution)/shard_map/all_to_all | solution.py:113
  176.4 6.4 all-to-all-start.1
  182.8 24.6 %copy.23 = bf16[6912,1280]{1,0:T(8,128)(2,1)} copy(bf16[6912,1280]{0,1:T(8,128)(2,1)} %bitcast.21) | data formatting | bytes 35389440 | tf_op jit(solution)/shard_map/transpose | solution.py:95
  207.4 12.5 %slice.24 = bf16[4,1344,1280]{2,1,0:T(8,128)(2,1)} slice(bf16[4,1728,1280]{2,1,0:T(8,128)(2,1)} %bitcast.16), slice={[0:4], [0:1344], [0:1280]} | slice | bytes 27525120 | tf_op jit(solution)/shard_map/slice | solution.py:109
  220.0 250.1 %all-to-all-done.1.block_ref = bf16[4,1296,1280]{2,1,0:T(8,128)(2,1)} async-done(((bf16[4,1296,1280]{2,1,0:T(8,128)(2,1)}), bf16[4,1296,1280]{2,1,0:T(8,128)(2,1)}, u32[]{:S(2)}, u32[]{:S(2)}) %all-to-all-start.1) | async-done | bytes 13271072 | tf_op jit(solution)/shard_map/all_to_all | solution.py:113
  470.1 6.5 all-to-all-start.2
  476.6 4.3 slice.27
  480.9 293.5 %all-to-all-done.2.block_ref = bf16[4,1344,1280]{2,1,0:T(8,128)(2,1)} async-done(((bf16[4,1344,1280]{2,1,0:T(8,128)(2,1)}), bf16[4,1344,1280]{2,1,0:T(8,128)(2,1)}, u32[]{:S(2)}, u32[]{:S(2)}) %all-to-all-start.2) | async-done | bytes 13762592 | tf_op jit(solution)/shard_map/all_to_all | solution.py:113
  774.4 4.8 all-to-all-start.3
  779.2 1.1 constant_dynamic-slice_fusion
  780.3 0.3 copy.28
  780.6 0.3 copy.27
  780.9 9.1 %shard_map.119 = (bf16[1728,5120]{1,0:T(8,128)(2,1)}, f32[432,1]{1,0:T(8,128)S(1)}) custom-call(bf16[4,432,1280]{2,1,0:T(8,128)(2,1)} %all-to-all-done.block_ref, bf16[32,5120]{1,0:T(8,128)(2,1)S(1)} %get-tuple-element.42.low_ref, bf16[1728,32]{1,0:T(8,128)(2,1)S(1)} %bitcast.10), custom_call_target="tpu_custom_call" | custom-call | flops 141557760 | bytes 8847360 | tf_op jit(solution)/shard_map/pallas_call | solution.py:49
  790.0 0.1 reduce.1
  790.1 24.5 %shard_map.120 = (bf16[1728,5120]{1,0:T(8,128)(2,1)}, f32[1296,1]{1,0:T(8,128)S(1)}) custom-call(bf16[4,1296,1280]{2,1,0:T(8,128)(2,1)} %all-to-all-done.1.block_ref, bf16[32,5120]{1,0:T(8,128)(2,1)S(1)} %get-tuple-element.42.low_ref, bf16[1728,32]{1,0:T(8,128)(2,1)S(1)} %bitcast.11, ...), custom_call_target="tpu_custom_call", output_to_operand_aliasing={{0}: (3, {})} | custom-call | flops 424673280 | bytes 26542080 | tf_op jit(solution)/shard_map/pallas_call | solution.py:49
  814.6 0.3 reduce.2
  814.9 0.7 pad_maximum_fusion.1
  815.6 25.0 %shard_map.121 = (bf16[1728,5120]{1,0:T(8,128)(2,1)}, f32[1344,1]{1,0:T(8,128)S(1)}) custom-call(bf16[4,1344,1280]{2,1,0:T(8,128)(2,1)} %all-to-all-done.2.block_ref, bf16[32,5120]{1,0:T(8,128)(2,1)S(1)} %get-tuple-element.41.low_ref, bf16[1728,32]{1,0:T(8,128)(2,1)S(1)} %bitcast.12), custom_call_target="tpu_custom_call" | custom-call | flops 440401920 | bytes 27525120 | tf_op jit(solution)/shard_map/pallas_call | solution.py:49
  840.6 0.3 reduce.3
  840.9 25.5 %all-to-all-done.3.block_ref = bf16[4,384,1280]{2,1,0:T(8,128)(2,1)} async-done(((bf16[4,384,1280]{2,1,0:T(8,128)(2,1)}), bf16[4,384,1280]{2,1,0:T(8,128)(2,1)}, u32[]{:S(2)}, u32[]{:S(2)}) %all-to-all-start.3) | async-done | bytes 3932192 | tf_op jit(solution)/shard_map/all_to_all | solution.py:113
  866.3 8.0 shard_map.122
  874.3 0.1 reduce.4
  874.4 0.7 pad_maximum_fusion.2
  (2 shorter events, 0.1 us)
Async XLA Ops:
  82.4 94.1 %all-to-all-start = ((bf16[4,432,1280]{2,1,0:T(8,128)(2,1)}), bf16[4,432,1280]{2,1,0:T(8,128)(2,1)}, u32[]{:S(2)}, u32[]{:S(2)}) async-start(bf16[4,432,1280]{2,1,0:T(8,128)(2,1)} %slice.26), calls=%async_computation | async-start | bytes 8847360 | tf_op jit(solution)/shard_map/all_to_all | solution.py:113
  176.4 293.7 %all-to-all-start.1 = ((bf16[4,1296,1280]{2,1,0:T(8,128)(2,1)}), bf16[4,1296,1280]{2,1,0:T(8,128)(2,1)}, u32[]{:S(2)}, u32[]{:S(2)}) async-start(bf16[4,1296,1280]{2,1,0:T(8,128)(2,1)} %slice.25), calls=%async_computation.1 | async-start | bytes 26542080 | tf_op jit(solution)/shard_map/all_to_all | solution.py:113
  470.1 304.3 %all-to-all-start.2 = ((bf16[4,1344,1280]{2,1,0:T(8,128)(2,1)}), bf16[4,1344,1280]{2,1,0:T(8,128)(2,1)}, u32[]{:S(2)}, u32[]{:S(2)}) async-start(bf16[4,1344,1280]{2,1,0:T(8,128)(2,1)} %slice.24), calls=%async_computation.2 | async-start | bytes 27525120 | tf_op jit(solution)/shard_map/all_to_all | solution.py:113
  774.4 91.9 %all-to-all-start.3 = ((bf16[4,384,1280]{2,1,0:T(8,128)(2,1)}), bf16[4,384,1280]{2,1,0:T(8,128)(2,1)}, u32[]{:S(2)}, u32[]{:S(2)}) async-start(bf16[4,384,1280]{2,1,0:T(8,128)(2,1)} %slice.27), calls=%async_computation.3 | async-start | bytes 7864320 | tf_op jit(solution)/shard_map/all_to_all | solution.py:113
